TPU v7x, 32 devices: a whole 2x2x4 slice. The times are simulated.
32 devices in a mesh: dp: 8 (over z, x), mp: 4 (over y, core).
Axes of the slice: x: 2, y: 2, z: 4, core: 2. Of those that a mesh axis runs over, the one named last changes fastest.
Arguments:
- text_in: bfloat16 [7680, 768], P(('dp', 'mp')), may hold values from -6 to 6
- caption_ids: int32 [480, 16], P('dp'), may hold values from 0 to 31999, as said below
- pairing: int32 [480], replicated, may hold values from 0 to 479, each once
- image_low: bfloat16 [19200, 768], P(('dp', 'mp')), may hold values from -6 to 6
- image_high: bfloat16 [13920, 768], P(('dp', 'mp')), may hold values from -6 to 6
- img_gains: float32 [2, 768], replicated, may hold values from 0.5 to 1.5
- img_qkv: bfloat16 [3, 768, 768], P(None, None, 'mp'), may hold values from -0.21875 to 0.21875
- img_out: bfloat16 [768, 768], P('mp'), may hold values from -0.625 to 0.625
- img_fc1: bfloat16 [768, 3072], P(None, 'mp'), may hold values from -0.21875 to 0.21875
- img_fc2: bfloat16 [3072, 768], P('mp'), may hold values from -0.109375 to 0.109375
- txt_qkv: bfloat16 [3, 768, 768], P(None, None, 'mp'), may hold values from -0.21875 to 0.21875
- txt_qv_bias: float32 [2, 768], P(None, 'mp'), may hold values from -3 to 3
- txt_out: bfloat16 [768, 768], P('mp'), may hold values from -0.4375 to 0.4375
- txt_fc1: bfloat16 [768, 3072], P(None, 'mp'), may hold values from -0.21875 to 0.21875
- txt_fc1_bias: float32 [3072], P('mp'), may hold values from -3 to 3
- txt_fc2: bfloat16 [3072, 768], P('mp'), may hold values from -0.109375 to 0.109375
- txt_gains: float32 [2, 768], replicated, may hold values from 0.5 to 1.5
- txt_shifts: float32 [2, 768], replicated, may hold values from -2 to 2
- txt_biases: float32 [2, 768], replicated, may hold values from -2 to 2
Outputs:
- loss: float32 [], replicated
- grad_text_in: float32 [7680, 768], P(('dp', 'mp'))
- grad_qkv: float32 [3, 768, 768], P(None, None, 'mp')
- grad_qv_bias: float32 [2, 768], P(None, 'mp')
- grad_out: float32 [768, 768], P('mp')
- grad_fc1: float32 [768, 3072], P(None, 'mp')
- grad_fc1_bias: float32 [3072], P('mp')
- grad_fc2: float32 [3072, 768], P('mp')
- grad_gains: float32 [2, 768], replicated
- grad_shifts: float32 [2, 768], replicated
- grad_biases: float32 [2, 768], replicated
Inputs may be any that keep to these rules, and one draw needn't show every extreme that they name: `caption_ids`: in each caption the nonzero ids come first and the zeros after; each caption has 4 to 16 nonzero ids. Image i is paired with caption pairing[i]; each caption is paired once.
All inputs are finite; a program needn't handle non-finite values.
Results may differ from a plain program's by a relative error of at most 0.017.
Values may be sent and summed in bfloat16 or wider, within the bound.
A program may use at most 192 MiB of HBM per device.

v0:
```python
import jax
import jax.numpy as jnp
from jax import lax
from jax.sharding import PartitionSpec as P

D = 768
HEAD = 64
L = 16
P_LOW = 50
P_HIGH = 145
EPS = 1e-06
SCALE = 40.0
LOSS_SCALE = 16.0
MASKED = -1e30


def layer_stats(values):
    center = values - jnp.mean(values, -1, keepdims=True)
    inverse = lax.rsqrt(jnp.mean(center * center, -1, keepdims=True) + EPS)
    return (center * inverse, inverse)


def norm_back(grad_out, unit, inverse, gain):
    scaled = grad_out * gain
    return inverse * (
        scaled
        - jnp.mean(scaled, -1, keepdims=True)
        - unit * jnp.mean(scaled * unit, -1, keepdims=True)
    )


def gelu_exact(values):
    return jax.nn.gelu(values, approximate=False)


def score_rows(queries, keys_all, keep):
    scores = (
        jnp.einsum("nqhe,nkhe->nhqk", queries, keys_all, preferred_element_type=jnp.float32) * 0.125
    )
    if keep is not None:
        scores = jnp.where(keep, scores, MASKED)
    return scores


def attention_shares(queries, keys_all, keep):
    scores = score_rows(queries, keys_all, keep)
    highest = jnp.max(scores, -1, keepdims=True)
    raised = jnp.exp(scores - highest)
    totals = jnp.sum(raised, -1, keepdims=True)
    return (raised / totals, highest + jnp.log(totals))


def image_tower(tokens, count, length, gains, weights):
    w_qkv, w_out, w_fc1, w_fc2 = weights
    head_count = D // HEAD
    inputs = tokens.astype(jnp.float32)
    unit, spare = layer_stats(inputs)
    normed = (unit * gains[0]).astype(jnp.bfloat16)
    projected = jnp.einsum("rd,jdw->jrw", normed, w_qkv, preferred_element_type=jnp.float32).astype(
        jnp.bfloat16
    )
    shaped = projected.reshape(3, count, length, head_count, HEAD)
    shares, spare_lse = attention_shares(shaped[0], shaped[1], None)
    context = jnp.einsum(
        "nhqk,nkhe->nqhe",
        shares.astype(jnp.bfloat16),
        shaped[2],
        preferred_element_type=jnp.float32,
    )
    context = context.astype(jnp.bfloat16).reshape(count * length, D)
    middle = inputs + jnp.dot(context, w_out, preferred_element_type=jnp.float32)
    unit2, spare2 = layer_stats(middle)
    normed2 = (unit2 * gains[1]).astype(jnp.bfloat16)
    active = gelu_exact(jnp.dot(normed2, w_fc1, preferred_element_type=jnp.float32)).astype(
        jnp.bfloat16
    )
    result = middle + jnp.dot(active, w_fc2, preferred_element_type=jnp.float32)
    pooled = jnp.mean(result.reshape(count, length, D), 1)
    return (pooled * lax.rsqrt(jnp.sum(pooled * pooled, -1, keepdims=True) + EPS)).astype(
        jnp.bfloat16
    )


def local(
    text_in,
    caption_ids,
    pairing,
    image_low,
    image_high,
    img_gains,
    img_qkv,
    img_out,
    img_fc1,
    img_fc2,
    txt_qkv,
    txt_qv_bias,
    txt_out,
    txt_fc1,
    txt_fc1_bias,
    txt_fc2,
    txt_gains,
    txt_shifts,
    txt_biases,
):
    weights = (
        lax.all_gather(img_qkv, "mp", axis=2, tiled=True),
        lax.all_gather(img_out, "mp", axis=0, tiled=True),
        lax.all_gather(img_fc1, "mp", axis=1, tiled=True),
        lax.all_gather(img_fc2, "mp", axis=0, tiled=True),
    )
    low_count = image_low.shape[0] // P_LOW
    high_count = image_high.shape[0] // P_HIGH
    images16 = jnp.concatenate(
        [
            image_tower(image_low, low_count, P_LOW, img_gains, weights),
            image_tower(image_high, high_count, P_HIGH, img_gains, weights),
        ],
        0,
    )
    width = txt_qkv.shape[2]
    head_count = width // HEAD
    own_rows = text_in.shape[0]
    own_caps = own_rows // L
    group_caps = caption_ids.shape[0]
    group_rows = group_caps * L
    own_ids = lax.dynamic_slice_in_dim(caption_ids, lax.axis_index("mp") * own_caps, own_caps, 0)
    keep = (caption_ids > 0)[:, None, None, :]
    inputs = text_in.astype(jnp.float32)
    unit1, inverse1 = layer_stats(inputs)
    normed1 = (unit1 * txt_gains[0] + txt_shifts[0]).astype(jnp.bfloat16)
    bias_rows = jnp.stack([txt_qv_bias[0], jnp.zeros_like(txt_qv_bias[0]), txt_qv_bias[1]])
    piece = lax.all_gather(normed1, "mp", axis=0, tiled=True)
    made = jnp.einsum("rd,jdw->rjw", piece, txt_qkv, preferred_element_type=jnp.float32) + bias_rows
    joined = jnp.concatenate(
        [piece, made.astype(jnp.bfloat16).reshape(piece.shape[0], 3 * width)], 1
    )
    normed1_all = joined[:, :D]
    triple = joined[:, D:].reshape(group_caps, L, 3, head_count, HEAD)
    queries = triple[:, :, 0]
    keys_all = triple[:, :, 1]
    values_all = triple[:, :, 2]
    shares, log_totals = attention_shares(queries, keys_all, keep)
    context = jnp.einsum(
        "nhqk,nkhe->nqhe",
        shares.astype(jnp.bfloat16),
        values_all,
        preferred_element_type=jnp.float32,
    )
    context = context.astype(jnp.bfloat16).reshape(group_rows, width)
    middle = inputs + (
        lax.psum_scatter(
            jnp.dot(context, txt_out, preferred_element_type=jnp.float32).astype(jnp.bfloat16),
            "mp",
            scatter_dimension=0,
            tiled=True,
        ).astype(jnp.float32)
        + txt_biases[0]
    )
    unit2, inverse2 = layer_stats(middle)
    normed2 = (unit2 * txt_gains[1] + txt_shifts[1]).astype(jnp.bfloat16)
    piece = lax.all_gather(normed2, "mp", axis=0, tiled=True)
    hidden_piece = jnp.dot(piece, txt_fc1, preferred_element_type=jnp.float32) + txt_fc1_bias
    spread = jnp.concatenate([piece.astype(jnp.float32), hidden_piece], 1)
    normed2_all = spread[:, :D].astype(jnp.bfloat16)
    hidden = spread[:, D:]
    active, gelu_pull = jax.vjp(gelu_exact, hidden)
    active16 = active.astype(jnp.bfloat16)
    result = middle + (
        lax.psum_scatter(
            jnp.dot(active16, txt_fc2, preferred_element_type=jnp.float32).astype(jnp.bfloat16),
            "mp",
            scatter_dimension=0,
            tiled=True,
        ).astype(jnp.float32)
        + txt_biases[1]
    )
    present = (own_ids > 0).astype(jnp.float32)
    counts = jnp.sum(present, 1, keepdims=True)
    pooled = jnp.sum(result.reshape(own_caps, L, D) * present[:, :, None], 1) / counts
    inverse_len = lax.rsqrt(jnp.sum(pooled * pooled, -1, keepdims=True) + EPS)
    captions_unit = pooled * inverse_len
    captions16 = captions_unit.astype(jnp.bfloat16)
    total_pairs = pairing.shape[0]
    first_pair = lax.axis_index(("dp", "mp")) * own_caps
    arrived = lax.all_gather(captions16, ("dp", "mp"), axis=0, tiled=True)
    logits = SCALE * jnp.einsum("id,jd->ij", images16, arrived, preferred_element_type=jnp.float32)
    targets = lax.dynamic_slice_in_dim(pairing, first_pair, own_caps, 0)
    matched = (targets[:, None] == jnp.arange(total_pairs)[None, :]).astype(jnp.float32)
    raised = jnp.exp(logits - SCALE)
    local_lse = SCALE + jnp.log(jnp.sum(raised, 1))
    partial_value = jnp.sum(raised, 0)
    own_term = 0.5 * jnp.sum(local_lse) - jnp.sum(matched * logits)
    summed, scalar = lax.psum((partial_value, own_term), ("dp", "mp"))
    other_lse = SCALE + jnp.log(summed)
    total = scalar + 0.5 * jnp.sum(other_lse)
    loss = total / total_pairs
    grads16 = (
        LOSS_SCALE
        * (
            0.5 * jnp.exp(logits - local_lse[:, None])
            + 0.5 * jnp.exp(logits - other_lse[None, :])
            - matched
        )
    ).astype(jnp.bfloat16)
    grad_caps = lax.psum_scatter(
        SCALE * jnp.einsum("ic,id->cd", grads16, images16, preferred_element_type=jnp.float32),
        ("dp", "mp"),
        scatter_dimension=0,
        tiled=True,
    )
    grad_pooled = inverse_len * (
        grad_caps - captions_unit * jnp.sum(captions_unit * grad_caps, -1, keepdims=True)
    )
    grad_result = (grad_pooled[:, None, :] * (present / counts)[:, :, None]).reshape(own_rows, D)
    grad_all = lax.all_gather(grad_result.astype(jnp.bfloat16), "mp", axis=0, tiled=True)
    grad_fc2 = jnp.einsum("gf,gd->fd", active16, grad_all, preferred_element_type=jnp.float32)
    grad_active = jnp.einsum("gd,fd->gf", grad_all, txt_fc2, preferred_element_type=jnp.float32)
    grad_hidden16 = gelu_pull(grad_active)[0].astype(jnp.bfloat16)
    grad_fc1 = jnp.einsum(
        "gd,gf->df", normed2_all, grad_hidden16, preferred_element_type=jnp.float32
    )
    grad_fc1_bias = jnp.sum(grad_hidden16.astype(jnp.float32), 0)
    grad_normed2 = lax.psum_scatter(
        jnp.einsum("gf,df->gd", grad_hidden16, txt_fc1, preferred_element_type=jnp.float32).astype(
            jnp.bfloat16
        ),
        "mp",
        scatter_dimension=0,
        tiled=True,
    ).astype(jnp.float32)
    grad_middle = grad_result + norm_back(grad_normed2, unit2, inverse2, txt_gains[1])
    grad_mid_all = lax.all_gather(grad_middle.astype(jnp.bfloat16), "mp", axis=0, tiled=True)
    grad_out = jnp.einsum("gw,gd->wd", context, grad_mid_all, preferred_element_type=jnp.float32)
    grad_context = jnp.einsum(
        "gd,wd->gw", grad_mid_all, txt_out, preferred_element_type=jnp.float32
    )
    grad_context = grad_context.astype(jnp.bfloat16).reshape(group_caps, L, head_count, HEAD)
    shares_again = jnp.exp(score_rows(queries, keys_all, keep) - log_totals)
    grad_shares = jnp.einsum(
        "nqhe,nkhe->nhqk", grad_context, values_all, preferred_element_type=jnp.float32
    )
    grad_values = jnp.einsum(
        "nhqk,nqhe->nkhe",
        shares_again.astype(jnp.bfloat16),
        grad_context,
        preferred_element_type=jnp.float32,
    ).astype(jnp.bfloat16)
    grad_scores = (
        shares_again * (grad_shares - jnp.sum(grad_shares * shares_again, -1, keepdims=True))
    ).astype(jnp.bfloat16)
    grad_queries = (
        jnp.einsum("nhqk,nkhe->nqhe", grad_scores, keys_all, preferred_element_type=jnp.float32)
        * 0.125
    ).astype(jnp.bfloat16)
    grad_keys = (
        jnp.einsum("nhqk,nqhe->nkhe", grad_scores, queries, preferred_element_type=jnp.float32)
        * 0.125
    ).astype(jnp.bfloat16)
    grad_triple = jnp.stack([grad_queries, grad_keys, grad_values], 0).reshape(3, group_rows, width)
    grad_qkv = jnp.einsum(
        "gd,jgw->jdw", normed1_all, grad_triple, preferred_element_type=jnp.float32
    )
    grad_qv_bias = jnp.stack(
        [
            jnp.sum(grad_triple[0].astype(jnp.float32), 0),
            jnp.sum(grad_triple[2].astype(jnp.float32), 0),
        ]
    )
    grad_normed1 = lax.psum_scatter(
        jnp.einsum("jgw,jdw->gd", grad_triple, txt_qkv, preferred_element_type=jnp.float32).astype(
            jnp.bfloat16
        ),
        "mp",
        scatter_dimension=0,
        tiled=True,
    ).astype(jnp.float32)
    grad_inputs = grad_middle + norm_back(grad_normed1, unit1, inverse1, txt_gains[0])
    summed_grads = lax.psum(
        (grad_qkv, grad_qv_bias, grad_out, grad_fc1, grad_fc1_bias, grad_fc2), "dp"
    )
    small_parts = jnp.stack(
        [
            jnp.sum(grad_normed1 * unit1, 0),
            jnp.sum(grad_normed2 * unit2, 0),
            jnp.sum(grad_normed1, 0),
            jnp.sum(grad_normed2, 0),
            jnp.sum(grad_middle, 0),
            jnp.sum(grad_result, 0),
        ]
    )
    shared = lax.psum(small_parts, ("dp", "mp"))
    return (
        loss,
        grad_inputs,
        summed_grads[0],
        summed_grads[1],
        summed_grads[2],
        summed_grads[3],
        summed_grads[4],
        summed_grads[5],
        shared[0:2],
        shared[2:4],
        shared[4:6],
    )


def solution(mesh):
    placed = (
        P(("dp", "mp"), None),
        P("dp", None),
        P(),
        P(("dp", "mp"), None),
        P(("dp", "mp"), None),
        P(),
        P(None, None, "mp"),
        P("mp", None),
        P(None, "mp"),
        P("mp", None),
        P(None, None, "mp"),
        P(None, "mp"),
        P("mp", None),
        P(None, "mp"),
        P("mp"),
        P("mp", None),
        P(),
        P(),
        P(),
    )
    return jax.shard_map(
        local,
        mesh=mesh,
        in_specs=placed,
        out_specs=(
            P(),
            P(("dp", "mp"), None),
            P(None, None, "mp"),
            P(None, "mp"),
            P("mp", None),
            P(None, "mp"),
            P("mp"),
            P("mp", None),
            P(),
            P(),
            P(),
        ),
        check_vma=False,
    )
```

profile of v0, /device:TPU:0, one launch (start us, length us, event | category | flops | bytes accessed | tf_op | source)
XLA Modules:
  0.0 829.3 jit_solution(6300139161258848959)
XLA Ops:
  14.9 20.2 %all-gather.18.cloned.1.call-done = bf16[960,768]{1,0:T(8,128)(2,1)} async-done(((bf16[240,768]{1,0:T(8,128)(2,1)}), bf16[960,768]{1,0:T(8,128)(2,1)}) %all-gather.18.cloned.1.call-update) | async-done | bytes 1474576 | tf_op jit(solution)/shard_map/all_gather | solution.py:132
  40.9 3.0 reshape_reshape.3
  43.9 3.2 fusion.221
  59.0 20.6 %reduce-scatter.7.cloned.1.call-done = bf16[240,768]{1,0:T(8,128)(2,1)} async-done(((bf16[960,768]{1,0:T(8,128)(2,1)}), bf16[240,768]{1,0:T(8,128)(2,1)}) %reduce-scatter.7.cloned.1.call-update) | async-done | bytes 368656 | tf_op jit(solution)/shard_map/reduce_scatter | solution.py:151
  84.2 27.8 %all-gather.10.cloned.1.call-done = bf16[3,768,768]{1,2,0:T(8,128)(2,1)} async-done(((bf16[3,768,192]{1,2,0:T(8,128)(2,1)}), bf16[3,768,768]{1,2,0:T(8,128)(2,1)}) %all-gather.10.cloned.1.call-update) | async-done | bytes 3538960 | tf_op jit(solution)/shard_map/all_gather | solution.py:106
  112.0 4.5 convert_bitcast_fusion
  117.9 4.5 squeeze.30
  122.4 4.1 squeeze.31
  126.5 3.8 fusion.45
  130.3 3.2 fusion.229
  136.3 4.5 convert_bitcast_fusion.1
  142.7 4.2 reshape.220
  156.6 3.3 reshape.237
  162.3 3.8 fusion.227
  168.5 4.1 fusion.69
  179.6 29.0 %all-gather.16.cloned.1.call-done = bf16[3072,768]{1,0:T(8,128)(2,1)} async-done(((bf16[768,768]{1,0:T(8,128)(2,1)}), bf16[3072,768]{1,0:T(8,128)(2,1)}) %all-gather.16.cloned.1.call-update) | async-done | bytes 4718608 | tf_op jit(solution)/shard_map/all_gather | solution.py:109
  208.6 25.3 %fusion.58 = f32[600,768]{1,0:T(8,128)S(1)} fusion(f32[600,768]{1,0:T(8,128)} %copy-done.23, bf16[3072,768]{1,0:T(8,128)(2,1)} %all-gather.16.cloned.1.call-done, bf16[768,3072]{1,0:T(8,128)(2,1)} %all-gather.14.cloned.1.call-done, f32[768]{0:T(1024)S(1)} %get-tuple-element.22, f32[600]{0:T(1024)S(1)} %add_rsqrt_fusion, f32[600]{0:T(1024)S(1)} %broadcast_multiply_fusion), kind=kOutput, calls=%fused_computation.102 | convolution fusion | flops 5784422400 | bytes 13131456 | tf_op jit(solution)/shard_map/dot_general | solution.py:77
  234.0 10.1 %multiply_convert_fusion = (bf16[960,768]{1,0:T(8,128)(2,1)S(1)}, f32[960,768]{1,0:T(8,128)}, f32[960,768]{1,0:T(8,128)}) fusion(f32[768]{0:T(1024)S(1)} %copy-done.64, bf16[960,768]{1,0:T(8,128)(2,1)} %all-gather.20.cloned.1.call-done, bf16[768,768]{1,0:T(8,128)(2,1)S(1)} %copy-done), kind=kOutput, calls=%fused_computation.54 | convolution fusion | flops 1181122560 | bytes 10030080 | tf_op jit(solution)/shard_map/dot_general | solution.py:162
  248.0 20.6 %fusion.62 = f32[435,768]{1,0:T(8,128)} fusion(f32[435,768]{1,0:T(8,128)} %copy-done.25, bf16[3072,768]{1,0:T(8,128)(2,1)} %all-gather.16.cloned.1.call-done, bf16[768,3072]{1,0:T(8,128)(2,1)} %all-gather.14.cloned.1.call-done, f32[768]{0:T(1024)S(1)} %get-tuple-element.22, f32[435]{0:T(512)S(1)} %add_rsqrt_fusion.2, f32[435]{0:T(512)S(1)} %broadcast_multiply_fusion.2), kind=kOutput, calls=%fused_computation.115 | convolution fusion | flops 4193706240 | bytes 12116376 | tf_op jit(solution)/shard_map/dot_general | solution.py:77
  277.0 42.7 %all-gather = bf16[32,15,768]{2,1,0:T(8,128)(2,1)S(1)} all-gather(bf16[1,15,768]{2,1,0:T(8,128)(2,1)S(1)} %fusion.139), channel_id=1, replica_groups=mesh['dp'=8,'mp'=4] {'dp','mp'}, dimensions={0}, use_global_device_ids=true | all-gather | bytes 760320 | tf_op jit(solution)/shard_map/all_gather | solution.py:185
  321.5 36.8 %psum.64 = f32[480]{0:T(512)S(1)} all-reduce(f32[480]{0:T(512)S(1)} %get-tuple-element.19), channel_id=1, replica_groups=mesh['dp'=8,'mp'=4] {'dp','mp'}, use_global_device_ids=true, to_apply=%region_32.33 | all-reduce | flops 480 | bytes 3840 | tf_op jit(solution)/shard_map/psum | solution.py:193
  360.7 77.1 %fusion = f32[16,768]{1,0:T(8,128)S(1)} fusion(f32[480,768]{1,0:T(8,128)S(1)} %convolution_multiply_fusion), kind=kCustom, calls=%all-reduce-scatter | all-reduce-scatter fusion | flops 393217 | bytes 1523712
  445.0 18.3 %all-gather.22.cloned.1.call-done = bf16[960,768]{1,0:T(8,128)(2,1)} async-done(((bf16[240,768]{1,0:T(8,128)(2,1)}), bf16[960,768]{1,0:T(8,128)(2,1)}) %all-gather.22.cloned.1.call-update) | async-done | bytes 1474576 | tf_op jit(solution)/shard_map/all_gather | solution.py:215
  463.3 5.6 convert_reduce_fusion
  472.6 27.5 %reduce-scatter.11.cloned.1.call-done = bf16[240,768]{1,0:T(8,128)(2,1)} async-done(((bf16[960,768]{1,0:T(8,128)(2,1)}), bf16[240,768]{1,0:T(8,128)(2,1)}) %reduce-scatter.11.cloned.1.call-update) | async-done | bytes 368656 | tf_op jit(solution)/shard_map/reduce_scatter | solution.py:223
  505.8 18.1 %all-gather.24.cloned.1.call-done = bf16[960,768]{1,0:T(8,128)(2,1)} async-done(((bf16[240,768]{1,0:T(8,128)(2,1)}), bf16[960,768]{1,0:T(8,128)(2,1)}) %all-gather.24.cloned.1.call-update) | async-done | bytes 1474576 | tf_op jit(solution)/shard_map/all_gather | solution.py:232
  545.4 3.9 bitcast_convert_fusion
  549.6 4.8 fusion.234
  563.4 13.5 %reduce-scatter.13.cloned.1.call-done = bf16[240,768]{1,0:T(8,128)(2,1)} async-done(((bf16[960,768]{1,0:T(8,128)(2,1)}), bf16[240,768]{1,0:T(8,128)(2,1)}) %reduce-scatter.13.cloned.1.call-update) | async-done | bytes 368656 | tf_op jit(solution)/shard_map/reduce_scatter | solution.py:269
  578.4 23.1 %all-reduce.3 = (f32[2,192]{1,0:T(2,128)}, f32[768]{0:T(1024)}) all-reduce(f32[2,192]{1,0:T(2,128)S(1)} %pad_maximum_fusion.7, f32[768]{0:T(1024)S(1)} %get-tuple-element.38), channel_id=1, replica_groups=mesh['dp'=8,'mp'=4] {'dp'}, use_global_device_ids=true, to_apply=%region_46.47 | all-reduce | flops 1152 | bytes 9216 | tf_op jit(solution)/shard_map/psum | solution.py:278
  601.5 41.9 %all-reduce.2 = (f32[]{:T(128)}, f32[6,768]{1,0:T(8,128)S(1)}) all-reduce(f32[]{:T(128)S(6)} %sub.157, f32[6,768]{1,0:T(8,128)S(1)} %stack.59), channel_id=1, replica_groups=mesh['dp'=8,'mp'=4] {'dp','mp'}, use_global_device_ids=true, to_apply=%region_30.31 | all-reduce | flops 4609 | bytes 36872 | tf_op jit(solution)/shard_map/psum | solution.py:193
  646.8 168.1 %all-reduce.7.cloned.1.call-done = (f32[3,768,192]{1,2,0:T(8,128)}, f32[192,768]{1,0:T(8,128)}, f32[768,768]{1,0:T(8,128)}, f32[768,768]{1,0:T(8,128)}) async-done(((f32[3,768,192]{1,2,0:T(8,128)}, f32[192,768]{1,0:T(8,128)}, f32[768,768]{1,0:T(8,128)}, f32[768,768]{1,0:T(8,128)}), (f32[3,768,192]{1,2,0:T(8,128)}, f32[192,768]{1,0:T(8,128)}, f32[768,768]{1,0:T(8,128)}, ...) | async-done | bytes 7077904 | tf_op jit(solution)/shard_map/psum | solution.py:278
  (302 shorter events, 129.2 us)
Async XLA Ops:
  7.2 226.8 %copy-start = (bf16[768,768]{1,0:T(8,128)(2,1)S(1)}, bf16[768,768]{1,0:T(8,128)(2,1)}, u32[]{:S(2)}) copy-start(bf16[768,768]{1,0:T(8,128)(2,1)} %param.32) | copy-start | bytes 3538948
  7.2 27.9 %all-gather.18.cloned.1.call-start = ((), (), s32[]{:S(2)}) async-start(), calls=%async_computation.8 | async-start | bytes 1843200 | tf_op jit(solution)/shard_map/all_gather | solution.py:132
  10.5 71.6 %copy-start.43 = (f32[768]{0:T(1024)}, f32[768]{0:T(1024)S(1)}, u32[]{:S(2)}) copy-start(f32[768]{0:T(1024)S(1)} %get-tuple-element.82) | copy-start | bytes 9220
  13.1 66.5 %reduce-scatter.7.cloned.1.call-start = ((), (), s32[]{:S(2)}) async-start(), calls=%async_computation.9 | async-start | bytes 1843200 | tf_op jit(solution)/shard_map/reduce_scatter | solution.py:151
  52.1 59.9 %all-gather.10.cloned.1.call-start = ((), (), s32[]{:S(2)}) async-start(), calls=%async_computation.4 | async-start | bytes 4423680 | tf_op jit(solution)/shard_map/all_gather | solution.py:106
  52.9 26.8 %copy-start.1 = (bf16[240,768]{1,0:T(8,128)(2,1)S(1)}, bf16[240,768]{1,0:T(8,128)(2,1)}, u32[]{:S(2)}) copy-start(bf16[240,768]{1,0:T(8,128)(2,1)} %param.19) | copy-start | bytes 1105924
  52.9 94.1 %all-gather.12.cloned.1.call-start = ((), (), s32[]{:S(2)}) async-start(), calls=%async_computation.5 | async-start | bytes 1474560 | tf_op jit(solution)/shard_map/all_gather | solution.py:107
  53.4 126.2 %all-gather.14.cloned.1.call-start = ((), (), s32[]{:S(2)}) async-start(), calls=%async_computation.6 | async-start | bytes 5898240 | tf_op jit(solution)/shard_map/all_gather | solution.py:108
  54.0 154.6 %all-gather.16.cloned.1.call-start = ((), (), s32[]{:S(2)}) async-start(), calls=%async_computation.7 | async-start | bytes 5898240 | tf_op jit(solution)/shard_map/all_gather | solution.py:109
  54.6 179.4 %all-gather.20.cloned.1.call-start = ((), (), s32[]{:S(2)}) async-start(), calls=%async_computation.10 | async-start | bytes 1843200 | tf_op jit(solution)/shard_map/all_gather | solution.py:161
  57.9 26.2 %copy-start.38 = (f32[768]{0:T(1024)}, f32[768]{0:T(1024)S(1)}, u32[]{:S(2)}) copy-start(f32[768]{0:T(1024)S(1)} %get-tuple-element.25) | copy-start | bytes 9220
  80.8 35.6 %copy-start.49 = (f32[240]{0:T(256)}, f32[240]{0:T(256)S(1)}, u32[]{:S(2)}) copy-start(f32[240]{0:T(256)S(1)} %broadcast_multiply_fusion.8) | copy-start | bytes 2884
  82.1 34.4 %copy-start.54 = (f32[240]{0:T(256)}, f32[240]{0:T(256)S(1)}, u32[]{:S(2)}) copy-start(f32[240]{0:T(256)S(1)} %add_rsqrt_fusion.4) | copy-start | bytes 2884
  84.1 191.2 %reduce-scatter.9.cloned.1.call-start = ((), (), s32[]{:S(2)}) async-start(), calls=%async_computation.11 | async-start | bytes 1843200 | tf_op jit(solution)/shard_map/reduce_scatter | solution.py:169
  208.6 25.4 %copy-start.64 = (f32[768]{0:T(1024)S(1)}, f32[768]{0:T(1024)}, u32[]{:S(2)}) copy-start(f32[768]{0:T(1024)} %param.33) | copy-start | bytes 9220
  247.7 215.6 %all-gather.22.cloned.1.call-start = ((), (), s32[]{:S(2)}) async-start(), calls=%async_computation.12 | async-start | bytes 1843200 | tf_op jit(solution)/shard_map/all_gather | solution.py:215
  276.9 42.8 %copy-start.59 = (f32[15]{0:T(128)}, f32[15]{0:T(128)S(1)}, u32[]{:S(2)}) copy-start(f32[15]{0:T(128)S(1)} %add_rsqrt_fusion.6) | copy-start | bytes 184
  437.9 4.3 collective-permute-start
  439.2 3.0 collective-permute-start.1
  444.1 57.5 %copy-start.28 = (f32[15,768]{1,0:T(8,128)}, f32[15,768]{1,0:T(8,128)S(1)}, u32[]{:S(2)}) copy-start(f32[15,768]{1,0:T(8,128)S(1)} %subtract_multiply_fusion.1) | copy-start | bytes 138244
  445.0 55.1 %reduce-scatter.11.cloned.1.call-start = ((), (), s32[]{:S(2)}) async-start(), calls=%async_computation.13 | async-start | bytes 1843200 | tf_op jit(solution)/shard_map/reduce_scatter | solution.py:223
  470.1 30.0 %copy-start.44 = (f32[768]{0:T(1024)S(1)}, f32[768]{0:T(1024)}, u32[]{:S(2)}) copy-start(f32[768]{0:T(1024)} %copy-done.43) | copy-start | bytes 9220
  470.1 30.0 %copy-start.50 = (f32[240]{0:T(256)S(1)}, f32[240]{0:T(256)}, u32[]{:S(2)}) copy-start(f32[240]{0:T(256)} %copy-done.49) | copy-start | bytes 2884
  470.1 30.0 %copy-start.55 = (f32[240]{0:T(256)S(1)}, f32[240]{0:T(256)}, u32[]{:S(2)}) copy-start(f32[240]{0:T(256)} %copy-done.54) | copy-start | bytes 2884
  472.5 32.6 %copy-start.32 = (f32[60,3,16]{2,1,0:T(4,128)S(1)}, f32[60,3,16]{2,1,0:T(4,128)}, u32[]{:S(2)}) copy-start(f32[60,3,16]{2,1,0:T(4,128)} %copy-done.31) | copy-start | bytes 34564
  472.5 32.6 %copy-start.34 = (f32[60,3,16]{2,1,0:T(4,128)S(1)}, f32[60,3,16]{2,1,0:T(4,128)}, u32[]{:S(2)}) copy-start(f32[60,3,16]{2,1,0:T(4,128)} %copy-done.33) | copy-start | bytes 34564
  472.6 51.4 %all-gather.24.cloned.1.call-start = ((), (), s32[]{:S(2)}) async-start(), calls=%async_computation.14 | async-start | bytes 1843200 | tf_op jit(solution)/shard_map/all_gather | solution.py:232
  503.9 25.1 %copy-start.4 = (f32[60,3,16,16]{2,3,1,0:T(8,128)S(1)}, f32[60,3,16,16]{2,3,1,0:T(8,128)}, u32[]{:S(2)}) copy-start(f32[60,3,16,16]{2,3,1,0:T(8,128)} %copy-done.3) | copy-start | bytes 552964
  504.7 72.2 %reduce-scatter.13.cloned.1.call-start = ((), (), s32[]{:S(2)}) async-start(), calls=%async_computation.15 | async-start | bytes 1843200 | tf_op jit(solution)/shard_map/reduce_scatter | solution.py:269
  549.4 265.5 %all-reduce.7.cloned.1.call-start = ((), (), s32[]{:S(2)}) async-start(), calls=%async_computation.16 | async-start | bytes 14155776 | tf_op jit(solution)/shard_map/psum | solution.py:278
  561.0 15.9 %copy-start.53 = (f32[240]{0:T(256)S(1)}, f32[240]{0:T(256)}, u32[]{:S(2)}) copy-start(f32[240]{0:T(256)} %copy-done.52) | copy-start | bytes 2884
  561.0 83.7 %copy-start.7 = (f32[240,768]{1,0:T(8,128)S(1)}, f32[240,768]{1,0:T(8,128)}, u32[]{:S(2)}) copy-start(f32[240,768]{1,0:T(8,128)} %copy-done.6) | copy-start | bytes 2211844
  (51 other events, 190.8 us)
Sparse Core Ops, SparseCore 0:
  13.2 21.7 all-gather.17
  52.2 27.3 reduce-scatter.6
  81.2 30.7 all-gather.9
  113.4 17.4 all-gather.11
  132.3 37.4 all-gather.13
  171.2 37.4 all-gather.15
  210.8 19.0 all-gather.19
  247.9 27.3 reduce-scatter.8
  445.1 18.2 all-gather.21
  472.7 27.3 reduce-scatter.10
  504.8 19.0 all-gather.23
  549.5 27.3 reduce-scatter.12
  581.9 232.9 all-reduce.6
where the time goes:
time: 839 us; the launch traced here: 829 us
  waiting for transfers between devices  347 us (41%)
  blocking collectives  222 us (26%)
  matrix products  125 us (15%)
  local copies, waits for them, and re-layouts  74.8 us (9%)
  other arithmetic  38.1 us (5%)
  between operations  18.9 us (2%)
    psum x1, waiting for transfers between devices, local(): lax.psum((grad_qkv, grad_qv_bias, grad_out, grad_fc1, grad_fc1_bias, grad...  168 us
    psum x2, blocking collectives, local(): summed, scalar = lax.psum((partial_value, own_term), ('dp', 'mp'))  78.7 us
    unnamed x1, blocking collectives  77.1 us
    dot_general x2, matrix products, image_tower(): result = middle + jnp.dot(active, w_fc2, preferred_element_type=jnp.float32)  45.9 us
    all_gather x1, blocking collectives, local(): arrived = lax.all_gather(captions16, ('dp', 'mp'), axis=0, tiled=True)  42.7 us
    all_gather x1, waiting for transfers between devices, local(): lax.all_gather(img_fc2, 'mp', axis=0, tiled=True)  29 us
    all_gather x1, waiting for transfers between devices, local(): lax.all_gather(img_qkv, 'mp', axis=2, tiled=True)  27.8 us
    reduce_scatter x1, waiting for transfers between devices, local(): lax.psum_scatter(jnp.einsum('gf,df->gd', grad_hidden16, txt_fc1, preferre...  27.5 us
  transfers between devices with their start and end apart: 15, of which 11 were waited for; matrix products, arithmetic and copies ran while one was open for 18% of the time, Pallas kernels for 0%

commit v1 on v0

--- a/solution.py
+++ b/solution.py
@@ -1,3 +1,4 @@
+import functools
 import jax
 import jax.numpy as jnp
 from jax import lax
@@ -12,6 +13,24 @@
 SCALE = 40.0
 LOSS_SCALE = 16.0
 MASKED = -1e30
+
+
+def tell_types_over_axis(local_array, named_axis):
+    local_next = lax.psum(1, axis_name=named_axis)
+    y_new = lax.axis_index(named_axis)
+    then, t1, b_now = (local_next, y_new, local_array.shape[0])
+    earlier, latest = (local_array, 1)
+    while latest < then:
+        x_now = lax.ppermute(
+            earlier, axis_name=named_axis, perm=[(kk, (kk - latest) % then) for kk in range(then)]
+        )
+        earlier = jnp.concatenate([earlier, x_now], 0)
+        latest = 2 * latest
+    tile_out = jnp.roll(earlier, t1 * b_now, 0)
+    return tile_out
+
+
+define_widths = functools.partial(tell_types_over_axis, named_axis="mp")
 
 
 def layer_stats(values):
@@ -106,7 +125,7 @@
         lax.all_gather(img_qkv, "mp", axis=2, tiled=True),
         lax.all_gather(img_out, "mp", axis=0, tiled=True),
         lax.all_gather(img_fc1, "mp", axis=1, tiled=True),
-        lax.all_gather(img_fc2, "mp", axis=0, tiled=True),
+        define_widths(img_fc2),
     )
     low_count = image_low.shape[0] // P_LOW
     high_count = image_high.shape[0] // P_HIGH

time: 839 us -> 861 us (1.026)
  local copies, waits for them, and re-layouts: 74.8 us -> 88.6 us
    ppermute x0 -> x2, waiting for transfers between devices: none -> 78.6 us  [tell_types_over_axis(): lax.ppermute(earlier, axis_name=named_axis, perm=[(kk, (kk - latest) % th...]
    all_gather x1 -> x0, waiting for transfers between devices: 29 us -> none  [local(): lax.all_gather(img_fc2, 'mp', axis=0, tiled=True)]
    all_gather x1, waiting for transfers between devices: 27.8 us -> 0.02 us  [local(): lax.all_gather(img_qkv, 'mp', axis=2, tiled=True)]
    reduce_scatter x1, waiting for transfers between devices: 20.6 us -> 0.01 us  [local(): lax.psum_scatter(jnp.dot(context, txt_out, preferred_element_type=jnp.flo...]
    unnamed x143 -> x162, local copies, waits for them, and re-layouts: 13.4 us -> 21.6 us
  transfers between devices with their start and end apart: 15 -> 16, of which waited for: 11 -> 10; matrix products, arithmetic and copies ran while one was open for 18% -> 19% of each run, Pallas kernels for 0% -> 0%
where the time goes in v1:
time: 861 us; the launch traced here: 851 us
  waiting for transfers between devices  348 us (40%)
  blocking collectives  221 us (26%)
  matrix products  125 us (15%)
  local copies, waits for them, and re-layouts  88.6 us (10%)
  other arithmetic  42.7 us (5%)
  between operations  19.3 us (2%)
    psum x1, waiting for transfers between devices, local(): lax.psum((grad_qkv, grad_qv_bias, grad_out, grad_fc1, grad_fc1_bias, grad...  168 us
    ppermute x2, waiting for transfers between devices, tell_types_over_axis(): lax.ppermute(earlier, axis_name=named_axis, perm=[(kk, (kk - latest) % th...  78.6 us
    psum x2, blocking collectives, local(): summed, scalar = lax.psum((partial_value, own_term), ('dp', 'mp'))  78.5 us
    unnamed x1, blocking collectives  77.1 us
    dot_general x2, matrix products, image_tower(): result = middle + jnp.dot(active, w_fc2, preferred_element_type=jnp.float32)  46.4 us
    all_gather x1, blocking collectives, local(): arrived = lax.all_gather(captions16, ('dp', 'mp'), axis=0, tiled=True)  42.7 us
    reduce_scatter x1, waiting for transfers between devices, local(): lax.psum_scatter(jnp.einsum('gf,df->gd', grad_hidden16, txt_fc1, preferre...  27.5 us
    psum x1, blocking collectives, local(): lax.psum((grad_qkv, grad_qv_bias, grad_out, grad_fc1, grad_fc1_bias, grad...  23.1 us
  transfers between devices with their start and end apart: 16, of which 10 were waited for; matrix products, arithmetic and copies ran while one was open for 19% of the time, Pallas kernels for 0%

profile of v1, /device:TPU:0, one launch (start us, length us, event | category | flops | bytes accessed | tf_op | source)
XLA Modules:
  0.0 851.0 jit_solution(17163631146982911660)
XLA Ops:
  14.9 20.2 %all-gather.15.cloned.1.call-done = bf16[960,768]{1,0:T(8,128)(2,1)} async-done(((bf16[240,768]{1,0:T(8,128)(2,1)}), bf16[960,768]{1,0:T(8,128)(2,1)}) %all-gather.15.cloned.1.call-update) | async-done | bytes 1474576 | tf_op jit(solution)/shard_map/all_gather | solution.py:151
  43.9 3.2 fusion.258
  54.3 13.7 %collective-permute-done = bf16[768,768]{1,0:T(8,128)(2,1)S(1)} collective-permute-done((bf16[768,768]{1,0:T(8,128)(2,1)S(1)}, bf16[768,768]{1,0:T(8,128)(2,1)S(1)}, u32[]{:S(2)}, u32[]{:S(2)}) %collective-permute-start) | collective-permute-done | bytes 1179680 | tf_op jit(solution)/shard_map/ppermute | solution.py:24
  83.6 64.9 %collective-permute-done.1 = bf16[1536,768]{1,0:T(8,128)(2,1)} collective-permute-done((bf16[1536,768]{1,0:T(8,128)(2,1)}, bf16[1536,768]{1,0:T(8,128)(2,1)}, u32[]{:S(2)}, u32[]{:S(2)}) %collective-permute-start.1) | collective-permute-done | bytes 2359328 | tf_op jit(solution)/shard_map/ppermute | solution.py:24
  148.5 3.2 constant_dynamic-update-slice_fusion.3
  153.9 3.3 constant_dynamic-update-slice_fusion
  161.9 4.7 convert_bitcast_fusion
  168.0 4.5 squeeze.30
  172.5 4.1 squeeze.31
  176.6 3.7 fusion.76
  180.3 3.2 fusion.266
  186.3 4.3 convert_bitcast_fusion.1
  192.4 4.2 reshape.220
  206.5 3.3 reshape.237
  212.2 3.8 fusion.264
  218.3 4.1 fusion.99
  229.4 25.6 %fusion.88 = f32[600,768]{1,0:T(8,128)S(1)} fusion(f32[600,768]{1,0:T(8,128)} %copy-done.25, bf16[6144,768]{1,0:T(8,128)(2,1)} %constant_dynamic-update-slice_fusion, s32[]{:T(128)S(6)} %select_n.25, bf16[768,3072]{1,0:T(8,128)(2,1)} %all-gather.13.cloned.1.call-done, f32[768]{0:T(1024)S(1)} %copy-done.63, f32[600]{0:T(1024)S(1)} %add_rsqrt_fusion, ...), kind=kOutput, calls=%fused_computation.132 | convolution fusion | flops 5784422400 | bytes 14974660 | tf_op jit(solution)/shard_map/dot_general | solution.py:96
  255.0 10.1 %multiply_convert_fusion = (bf16[960,768]{1,0:T(8,128)(2,1)S(1)}, f32[960,768]{1,0:T(8,128)}, f32[960,768]{1,0:T(8,128)}) fusion(f32[768]{0:T(1024)S(1)} %copy-done.71, bf16[960,768]{1,0:T(8,128)(2,1)} %all-gather.17.cloned.1.call-done, bf16[768,768]{1,0:T(8,128)(2,1)S(1)} %copy-done), kind=kOutput, calls=%fused_computation.57 | convolution fusion | flops 1181122560 | bytes 10030080 | tf_op jit(solution)/shard_map/dot_general | solution.py:181
  268.9 20.8 %fusion.102 = f32[435,768]{1,0:T(8,128)} fusion(f32[435,768]{1,0:T(8,128)} %copy-done.27, bf16[6144,768]{1,0:T(8,128)(2,1)} %constant_dynamic-update-slice_fusion, s32[]{:T(128)S(6)} %select_n.25, bf16[768,3072]{1,0:T(8,128)(2,1)} %all-gather.13.cloned.1.call-done, f32[768]{0:T(1024)S(1)} %copy-done.63, f32[435]{0:T(512)S(1)} %add_rsqrt_fusion.2, ...), kind=kOutput, calls=%fused_computation.152 | convolution fusion | flops 4193706240 | bytes 13483420 | tf_op jit(solution)/shard_map/dot_general | solution.py:96
  298.4 42.7 %all-gather = bf16[32,15,768]{2,1,0:T(8,128)(2,1)S(1)} all-gather(bf16[1,15,768]{2,1,0:T(8,128)(2,1)S(1)} %fusion.174), channel_id=1, replica_groups=mesh['dp'=8,'mp'=4] {'dp','mp'}, dimensions={0}, use_global_device_ids=true | all-gather | bytes 760320 | tf_op jit(solution)/shard_map/all_gather | solution.py:204
  342.9 36.8 %psum.64 = f32[480]{0:T(512)S(1)} all-reduce(f32[480]{0:T(512)S(1)} %get-tuple-element.19), channel_id=1, replica_groups=mesh['dp'=8,'mp'=4] {'dp','mp'}, use_global_device_ids=true, to_apply=%region_32.33 | all-reduce | flops 480 | bytes 3840 | tf_op jit(solution)/shard_map/psum | solution.py:212
  382.1 77.1 %fusion = f32[16,768]{1,0:T(8,128)S(1)} fusion(f32[480,768]{1,0:T(8,128)S(1)} %convolution_multiply_fusion), kind=kCustom, calls=%all-reduce-scatter | all-reduce-scatter fusion | flops 393217 | bytes 1523712
  466.4 18.3 %all-gather.19.cloned.1.call-done = bf16[960,768]{1,0:T(8,128)(2,1)} async-done(((bf16[240,768]{1,0:T(8,128)(2,1)}), bf16[960,768]{1,0:T(8,128)(2,1)}) %all-gather.19.cloned.1.call-update) | async-done | bytes 1474576 | tf_op jit(solution)/shard_map/all_gather | solution.py:234
  484.8 5.6 convert_reduce_fusion
  494.0 27.5 %reduce-scatter.11.cloned.1.call-done = bf16[240,768]{1,0:T(8,128)(2,1)} async-done(((bf16[960,768]{1,0:T(8,128)(2,1)}), bf16[240,768]{1,0:T(8,128)(2,1)}) %reduce-scatter.11.cloned.1.call-update) | async-done | bytes 368656 | tf_op jit(solution)/shard_map/reduce_scatter | solution.py:242
  527.3 18.1 %all-gather.21.cloned.1.call-done = bf16[960,768]{1,0:T(8,128)(2,1)} async-done(((bf16[240,768]{1,0:T(8,128)(2,1)}), bf16[960,768]{1,0:T(8,128)(2,1)}) %all-gather.21.cloned.1.call-update) | async-done | bytes 1474576 | tf_op jit(solution)/shard_map/all_gather | solution.py:251
  566.9 3.9 bitcast_convert_fusion
  571.1 4.8 fusion.271
  584.9 13.6 %reduce-scatter.13.cloned.1.call-done = bf16[240,768]{1,0:T(8,128)(2,1)} async-done(((bf16[960,768]{1,0:T(8,128)(2,1)}), bf16[240,768]{1,0:T(8,128)(2,1)}) %reduce-scatter.13.cloned.1.call-update) | async-done | bytes 368656 | tf_op jit(solution)/shard_map/reduce_scatter | solution.py:288
  600.0 23.1 %all-reduce.3 = (f32[2,192]{1,0:T(2,128)}, f32[768]{0:T(1024)}) all-reduce(f32[2,192]{1,0:T(2,128)S(1)} %pad_maximum_fusion.8, f32[768]{0:T(1024)S(1)} %get-tuple-element.38), channel_id=1, replica_groups=mesh['dp'=8,'mp'=4] {'dp'}, use_global_device_ids=true, to_apply=%region_46.47 | all-reduce | flops 1152 | bytes 9216 | tf_op jit(solution)/shard_map/psum | solution.py:297
  623.1 41.7 %all-reduce.2 = (f32[]{:T(128)}, f32[6,768]{1,0:T(8,128)S(1)}) all-reduce(f32[]{:T(128)S(6)} %sub.162, f32[6,768]{1,0:T(8,128)S(1)} %stack.59), channel_id=1, replica_groups=mesh['dp'=8,'mp'=4] {'dp','mp'}, use_global_device_ids=true, to_apply=%region_30.31 | all-reduce | flops 4609 | bytes 36872 | tf_op jit(solution)/shard_map/psum | solution.py:212
  668.2 168.0 %all-reduce.7.cloned.1.call-done = (f32[3,768,192]{1,2,0:T(8,128)}, f32[192,768]{1,0:T(8,128)}, f32[768,768]{1,0:T(8,128)}, f32[768,768]{1,0:T(8,128)}) async-done(((f32[3,768,192]{1,2,0:T(8,128)}, f32[192,768]{1,0:T(8,128)}, f32[768,768]{1,0:T(8,128)}, f32[768,768]{1,0:T(8,128)}), (f32[3,768,192]{1,2,0:T(8,128)}, f32[192,768]{1,0:T(8,128)}, f32[768,768]{1,0:T(8,128)}, ...) | async-done | bytes 7077904 | tf_op jit(solution)/shard_map/psum | solution.py:297
  (324 shorter events, 145.6 us)
Async XLA Ops:
  7.2 247.8 %copy-start = (bf16[768,768]{1,0:T(8,128)(2,1)S(1)}, bf16[768,768]{1,0:T(8,128)(2,1)}, u32[]{:S(2)}) copy-start(bf16[768,768]{1,0:T(8,128)(2,1)} %param.32) | copy-start | bytes 3538948
  7.2 27.9 %all-gather.15.cloned.1.call-start = ((), (), s32[]{:S(2)}) async-start(), calls=%async_computation.7 | async-start | bytes 1843200 | tf_op jit(solution)/shard_map/all_gather | solution.py:151
  10.5 149.2 %copy-start.45 = (f32[768]{0:T(1024)}, f32[768]{0:T(1024)S(1)}, u32[]{:S(2)}) copy-start(f32[768]{0:T(1024)S(1)} %get-tuple-element.82) | copy-start | bytes 9220
  13.1 144.2 %reduce-scatter.7.cloned.1.call-start = ((), (), s32[]{:S(2)}) async-start(), calls=%async_computation.8 | async-start | bytes 1843200 | tf_op jit(solution)/shard_map/reduce_scatter | solution.py:170
  52.1 109.7 %all-gather.9.cloned.1.call-start = ((), (), s32[]{:S(2)}) async-start(), calls=%async_computation.4 | async-start | bytes 4423680 | tf_op jit(solution)/shard_map/all_gather | solution.py:125
  52.9 143.8 %all-gather.11.cloned.1.call-start = ((), (), s32[]{:S(2)}) async-start(), calls=%async_computation.5 | async-start | bytes 1474560 | tf_op jit(solution)/shard_map/all_gather | solution.py:126
  53.4 175.9 %all-gather.13.cloned.1.call-start = ((), (), s32[]{:S(2)}) async-start(), calls=%async_computation.6 | async-start | bytes 5898240 | tf_op jit(solution)/shard_map/all_gather | solution.py:127
  54.0 200.9 %all-gather.17.cloned.1.call-start = ((), (), s32[]{:S(2)}) async-start(), calls=%async_computation.9 | async-start | bytes 1843200 | tf_op jit(solution)/shard_map/all_gather | solution.py:180
  54.1 13.9 %collective-permute-start = (bf16[768,768]{1,0:T(8,128)(2,1)S(1)}, bf16[768,768]{1,0:T(8,128)(2,1)S(1)}, u32[]{:S(2)}, u32[]{:S(2)}) collective-permute-start(bf16[768,768]{1,0:T(8,128)(2,1)S(1)} %copy-done.6), channel_id=1, source_target_pairs={{0,3},{1,0},{2,1},{3,2},{4,7},{5,4},{6,5},{7,6},{8,11},{9,8},{10,9... | collective-permute-start | bytes 3538952 | tf_op jit(solution)/shard_map/ppermute | solution.py:24
  69.6 78.9 %collective-permute-start.1 = (bf16[1536,768]{1,0:T(8,128)(2,1)}, bf16[1536,768]{1,0:T(8,128)(2,1)}, u32[]{:S(2)}, u32[]{:S(2)}) collective-permute-start(bf16[1536,768]{1,0:T(8,128)(2,1)} %pad_maximum_fusion), channel_id=1, source_target_pairs={{0,2},{1,3},{2,0},{3,1},{4,6},{5,7},{6,4},{7,5},{8,10},{9,11},{10,... | collective-permute-start | bytes 7077896 | tf_op jit(solution)/shard_map/ppermute | solution.py:24
  77.4 82.4 %copy-start.40 = (f32[768]{0:T(1024)}, f32[768]{0:T(1024)S(1)}, u32[]{:S(2)}) copy-start(f32[768]{0:T(1024)S(1)} %get-tuple-element.25) | copy-start | bytes 9220
  80.9 70.8 %copy-start.58 = (f32[600]{0:T(1024)}, f32[600]{0:T(1024)S(1)}, u32[]{:S(2)}) copy-start(f32[600]{0:T(1024)S(1)} %broadcast_multiply_fusion.1) | copy-start | bytes 7204
  161.7 135.0 %reduce-scatter.9.cloned.1.call-start = ((), (), s32[]{:S(2)}) async-start(), calls=%async_computation.10 | async-start | bytes 1843200 | tf_op jit(solution)/shard_map/reduce_scatter | solution.py:188
  229.4 25.6 %copy-start.71 = (f32[768]{0:T(1024)S(1)}, f32[768]{0:T(1024)}, u32[]{:S(2)}) copy-start(f32[768]{0:T(1024)} %param.33) | copy-start | bytes 9220
  268.7 216.1 %all-gather.19.cloned.1.call-start = ((), (), s32[]{:S(2)}) async-start(), calls=%async_computation.11 | async-start | bytes 1843200 | tf_op jit(solution)/shard_map/all_gather | solution.py:234
  298.3 42.8 %copy-start.62 = (f32[15]{0:T(128)}, f32[15]{0:T(128)S(1)}, u32[]{:S(2)}) copy-start(f32[15]{0:T(128)S(1)} %add_rsqrt_fusion.6) | copy-start | bytes 184
  459.3 4.3 collective-permute-start.2
  460.6 3.0 collective-permute-start.3
  465.5 57.5 %copy-start.30 = (f32[15,768]{1,0:T(8,128)}, f32[15,768]{1,0:T(8,128)S(1)}, u32[]{:S(2)}) copy-start(f32[15,768]{1,0:T(8,128)S(1)} %subtract_multiply_fusion.1) | copy-start | bytes 138244
  466.4 55.2 %reduce-scatter.11.cloned.1.call-start = ((), (), s32[]{:S(2)}) async-start(), calls=%async_computation.12 | async-start | bytes 1843200 | tf_op jit(solution)/shard_map/reduce_scatter | solution.py:242
  491.5 30.1 %copy-start.46 = (f32[768]{0:T(1024)S(1)}, f32[768]{0:T(1024)}, u32[]{:S(2)}) copy-start(f32[768]{0:T(1024)} %copy-done.45) | copy-start | bytes 9220
  491.5 30.1 %copy-start.51 = (f32[240]{0:T(256)S(1)}, f32[240]{0:T(256)}, u32[]{:S(2)}) copy-start(f32[240]{0:T(256)} %copy-done.50) | copy-start | bytes 2884
  491.5 30.1 %copy-start.56 = (f32[240]{0:T(256)S(1)}, f32[240]{0:T(256)}, u32[]{:S(2)}) copy-start(f32[240]{0:T(256)} %copy-done.55) | copy-start | bytes 2884
  493.9 32.7 %copy-start.34 = (f32[60,3,16]{2,1,0:T(4,128)S(1)}, f32[60,3,16]{2,1,0:T(4,128)}, u32[]{:S(2)}) copy-start(f32[60,3,16]{2,1,0:T(4,128)} %copy-done.33) | copy-start | bytes 34564
  493.9 32.7 %copy-start.36 = (f32[60,3,16]{2,1,0:T(4,128)S(1)}, f32[60,3,16]{2,1,0:T(4,128)}, u32[]{:S(2)}) copy-start(f32[60,3,16]{2,1,0:T(4,128)} %copy-done.35) | copy-start | bytes 34564
  494.0 51.5 %all-gather.21.cloned.1.call-start = ((), (), s32[]{:S(2)}) async-start(), calls=%async_computation.13 | async-start | bytes 1843200 | tf_op jit(solution)/shard_map/all_gather | solution.py:251
  525.4 25.1 %copy-start.4 = (f32[60,3,16,16]{2,3,1,0:T(8,128)S(1)}, f32[60,3,16,16]{2,3,1,0:T(8,128)}, u32[]{:S(2)}) copy-start(f32[60,3,16,16]{2,3,1,0:T(8,128)} %copy-done.3) | copy-start | bytes 552964
  526.2 72.3 %reduce-scatter.13.cloned.1.call-start = ((), (), s32[]{:S(2)}) async-start(), calls=%async_computation.14 | async-start | bytes 1843200 | tf_op jit(solution)/shard_map/reduce_scatter | solution.py:288
  570.9 265.4 %all-reduce.7.cloned.1.call-start = ((), (), s32[]{:S(2)}) async-start(), calls=%async_computation.15 | async-start | bytes 14155776 | tf_op jit(solution)/shard_map/psum | solution.py:297
  582.5 16.0 %copy-start.49 = (f32[240]{0:T(256)S(1)}, f32[240]{0:T(256)}, u32[]{:S(2)}) copy-start(f32[240]{0:T(256)} %copy-done.48) | copy-start | bytes 2884
  582.5 16.0 %copy-start.54 = (f32[240]{0:T(256)S(1)}, f32[240]{0:T(256)}, u32[]{:S(2)}) copy-start(f32[240]{0:T(256)} %copy-done.53) | copy-start | bytes 2884
  582.5 83.6 %copy-start.8 = (f32[240,768]{1,0:T(8,128)S(1)}, f32[240,768]{1,0:T(8,128)}, u32[]{:S(2)}) copy-start(f32[240,768]{1,0:T(8,128)} %copy-done.7) | copy-start | bytes 2211844
  (59 other events, 228.9 us)
Sparse Core Ops, SparseCore 0:
  13.2 21.7 all-gather.14
  52.2 32.4 reduce-scatter.6
  86.3 49.6 all-gather.8
  137.4 18.4 all-gather.10
  157.2 37.4 all-gather.12
  196.7 19.0 all-gather.16
  268.8 27.8 reduce-scatter.8
  466.5 18.2 all-gather.18
  494.1 27.3 reduce-scatter.10
  526.3 19.0 all-gather.20
  571.0 27.4 reduce-scatter.12
  603.3 232.9 all-reduce.6
